TPU v7x, 32 devices: a whole 2x2x4 slice. The times are simulated.
32 devices in a mesh: gx: 8 (over z, y), gy: 4 (over x, core).
Axes of the slice: x: 2, y: 2, z: 4, core: 2. Of those that a mesh axis runs over, the one named last changes fastest.
Arguments:
- goal_embed: bfloat16 [4096, 128], P(('gx', 'gy')), may hold values from -6 to 6
- goal_bins: int32 [4096], P(('gx', 'gy')), may hold values from 0 to 2047, as said below
- goal_weights: float32 [4096], P(('gx', 'gy')), may hold values from 0.1 to 10
Outputs:
- bin_mean: float32 [2048, 128], P(('gx', 'gy'))
- rarity: float32 [2048], P(('gx', 'gy'))
Inputs may be any that keep to these rules, and one draw needn't show every extreme that they name: `goal_bins`: bin b belongs to owner b // 64, owners numbered in the order of gx then gy. Of the goals of one device, at most 8 fall in the bins of one owner; some owner receives exactly 8 goals from every device.
All inputs are finite; a program needn't handle non-finite values.
Results may differ from a plain program's by a relative error of at most 0.0029.
Values may be sent and summed in bfloat16 or wider, within the bound.
No kernel may reach another device: no remote copies, remote signals or barrier semaphores. Data moves between devices by JAX's collectives and lax.ppermute only.
A program may use at most 64 MiB of HBM per device.

v0:
```python
import jax
import jax.numpy as jnp
from jax import lax
from jax.sharding import PartitionSpec as P

BINS_DEV = 64


def shards(goal_embed, goal_bins, goal_weights):
    scaled = (goal_weights[:, None] * goal_embed.astype(jnp.float32)).astype(jnp.bfloat16)
    width = goal_embed.shape[1]
    local_goals = goal_embed.shape[0]
    across = lax.axis_size("gx")
    along = lax.axis_size("gy")
    devices = across * along
    capacity = max(2, 2 * local_goals // devices)
    owners = goal_bins // BINS_DEV
    offsets = goal_bins - owners * BINS_DEV
    member = (owners[:, None] == jnp.arange(devices, dtype=jnp.int32)[None, :]).astype(jnp.int32)
    before = jnp.cumsum(member, axis=0) - member
    places = jnp.sum(before * member, axis=1)
    slots = owners * capacity + places
    outgoing = jnp.zeros((devices * capacity, width), jnp.bfloat16).at[slots].set(scaled)
    tagging = jnp.zeros((2, devices * capacity), jnp.float32)
    tagging = tagging.at[0, slots].set(goal_weights).at[1, slots].set(offsets.astype(jnp.float32))
    outgoing = outgoing.reshape(across, along, capacity, width)
    tagging = tagging.reshape(2, across, along, capacity)
    arrived = lax.all_to_all(
        lax.all_to_all(outgoing, "gx", split_axis=0, concat_axis=0, tiled=True),
        "gy",
        split_axis=1,
        concat_axis=1,
        tiled=True,
    )
    tag_rows = lax.all_to_all(
        lax.all_to_all(tagging, "gx", split_axis=1, concat_axis=1, tiled=True),
        "gy",
        split_axis=2,
        concat_axis=2,
        tiled=True,
    )
    arrived = arrived.reshape(devices * capacity, width)
    tag_rows = tag_rows.reshape(2, devices * capacity)
    labels = lax.broadcasted_iota(jnp.int32, (BINS_DEV, 1), 0).astype(jnp.float32)
    selector = tag_rows[1][None, :] == labels
    bin_sums = jnp.dot(selector.astype(jnp.bfloat16), arrived, preferred_element_type=jnp.float32)
    bin_mass = jnp.dot(selector.astype(jnp.float32), tag_rows[0], precision=lax.Precision.HIGHEST)
    total_mass = lax.psum(jnp.sum(bin_mass), ("gx", "gy"))
    bin_mean = bin_sums / (bin_mass[:, None] + 1.0)
    rarity = jnp.log(total_mass / (BINS_DEV * devices)) - jnp.log(bin_mass + 1.0)
    return (bin_mean, rarity)


def solution(mesh):
    in_specs = (P(("gx", "gy"), None), P(("gx", "gy")), P(("gx", "gy")))
    out_specs = (P(("gx", "gy"), None), P(("gx", "gy")))
    return jax.shard_map(shards, mesh=mesh, in_specs=in_specs, out_specs=out_specs, check_vma=False)
```

profile of v0, /device:TPU:0, one launch (start us, length us, event | category | flops | bytes accessed | tf_op | source)
XLA Modules:
  0.0 93.1 jit_solution(4781643750971819764)
XLA Ops:
  0.6 0.7 subtract_convert_fusion
  1.3 0.1 fusion.2
  1.4 0.2 reduce_window_sum.11
  1.6 0.2 select_reduce_fusion
  1.8 0.0 copy-start.1
  1.8 0.6 copy-done.1
  2.4 6.9 %scatter_fusion = f32[2,256]{1,0:T(2,128)S(1)} fusion(f32[2,256]{1,0:T(2,128)S(1)} %broadcast_in_dim.6, s32[128]{0:T(128)S(1)} %select_bitcast_fusion.1, f32[128]{0:T(128)S(1)} %copy-done.1), kind=kCustom, calls=%fused_computation | custom fusion | bytes 2560 | tf_op jit(solution)/shard_map/scatter | solution.py:25
  9.3 6.9 %scatter_fusion.1 = f32[2,256]{1,0:T(2,128)S(1)} fusion(f32[2,256]{1,0:T(2,128)S(1)} %scatter_fusion, s32[128]{0:T(128)S(1)} %get-tuple-element.4, f32[128]{0:T(128)S(1)} %get-tuple-element.2), kind=kCustom, calls=%fused_computation.1 | custom fusion | bytes 2560 | tf_op jit(solution)/shard_map/scatter | solution.py:25
  16.2 0.1 reshape.27
  16.3 13.8 %all_to_all.20 = f32[2,8,4,8]{3,2,0,1:T(4,128)S(1)} all-to-all(f32[2,8,4,8]{3,2,0,1:T(4,128)S(1)} %copy.14), channel_id=1, replica_groups=mesh['gx'=8,'gy'=4] {'gx'}, dimensions={1} | all-to-all | bytes 4096 | tf_op jit(solution)/shard_map/all_to_all | solution.py:36
  30.1 0.0 copy-start
  30.1 0.7 reshape.56
  30.8 3.2 %all-to-all-start.1 = ((f32[4,1,128]{2,1,0:T(1,128)}), f32[4,1,128]{2,1,0:T(1,128)S(1)}, u32[]{:S(2)}, u32[]{:S(2)}) async-start(f32[4,1,128]{2,1,0:T(1,128)} %reshape.56), calls=%async_computation.1 | async-start | bytes 4096 | tf_op jit(solution)/shard_map/all_to_all | solution.py:35
  34.0 0.0 copy-done
  34.0 1.5 %scatter_custom_fusion.2 = bf16[256,128]{1,0:T(8,128)(2,1)} fusion(s32[128]{0:T(128)S(1)} %get-tuple-element.5, bf16[128,128]{1,0:T(8,128)(2,1)S(1)} %copy-done, f32[128]{0:T(128)S(1)} %copy-done.1, bf16[]{:T(256)} %constant.38.clone.1), kind=kCustom, calls=%fused_computation.11 | custom fusion | flops 49152 | bytes 98818 | tf_op jit(solution)/shard_map/scatter | solution.py:23
  35.6 2.1 %all-to-all-done.1 = f32[4,1,128]{2,1,0:T(1,128)S(1)} async-done(((f32[4,1,128]{2,1,0:T(1,128)}), f32[4,1,128]{2,1,0:T(1,128)S(1)}, u32[]{:S(2)}, u32[]{:S(2)}) %all-to-all-start.1) | async-done | bytes 2080 | tf_op jit(solution)/shard_map/all_to_all | solution.py:35
  37.7 3.3 %all-to-all-start.2 = ((bf16[8,4,8,128]{3,2,1,0:T(8,128)(2,1)}), bf16[8,4,8,128]{3,2,1,0:T(8,128)(2,1)S(1)}, u32[]{:S(2)}, u32[]{:S(2)}) async-start(bf16[8,4,8,128]{3,2,1,0:T(8,128)(2,1)} %bitcast.3), calls=%async_computation.2 | async-start | bytes 131072 | tf_op jit(solution)/shard_map/all_to_all | solution.py:29
  41.0 0.5 broadcast.119
  41.6 0.7 reduce
  42.2 0.1 reshape.57
  42.3 0.1 eq.31
  42.5 0.1 reshape.51
  42.5 0.8 fusion.11
  43.4 39.9 %psum.7 = f32[]{:T(128)} all-reduce(f32[]{:T(128)} %get-tuple-element.10), channel_id=1, replica_groups=mesh['gx'=8,'gy'=4] {'gx','gy'}, use_global_device_ids=true, to_apply=%region_6.7 | all-reduce | flops 1 | bytes 8 | tf_op jit(solution)/shard_map/psum | solution.py:48
  84.0 0.0 all-to-all-done.2
  84.0 0.6 copy.17
  84.6 3.5 %all-to-all-start.3 = ((bf16[8,4,8,128]{3,2,0,1:T(8,128)(2,1)}), bf16[8,4,8,128]{3,2,0,1:T(8,128)(2,1)S(1)}, u32[]{:S(2)}, u32[]{:S(2)}) async-start(bf16[8,4,8,128]{3,2,0,1:T(8,128)(2,1)} %copy.17), calls=%async_computation.3 | async-start | bytes 131072 | tf_op jit(solution)/shard_map/all_to_all | solution.py:28
  88.1 0.5 log_subtract_fusion
  88.7 3.6 %all-to-all-done.3 = bf16[8,4,8,128]{3,2,0,1:T(8,128)(2,1)S(1)} async-done(((bf16[8,4,8,128]{3,2,0,1:T(8,128)(2,1)}), bf16[8,4,8,128]{3,2,0,1:T(8,128)(2,1)S(1)}, u32[]{:S(2)}, u32[]{:S(2)}) %all-to-all-start.3) | async-done | bytes 65568 | tf_op jit(solution)/shard_map/all_to_all | solution.py:28
  92.3 0.8 convolution_divide_fusion
  (10 shorter events, 0.1 us)
Async XLA Ops:
  1.8 0.7 copy-start.1
  30.1 3.9 %copy-start = (bf16[128,128]{1,0:T(8,128)(2,1)S(1)}, bf16[128,128]{1,0:T(8,128)(2,1)}, u32[]{:S(2)}) copy-start(bf16[128,128]{1,0:T(8,128)(2,1)} %param.3) | copy-start | bytes 98308
  30.8 6.9 %all-to-all-start.1 = ((f32[4,1,128]{2,1,0:T(1,128)}), f32[4,1,128]{2,1,0:T(1,128)S(1)}, u32[]{:S(2)}, u32[]{:S(2)}) async-start(f32[4,1,128]{2,1,0:T(1,128)} %reshape.56), calls=%async_computation.1 | async-start | bytes 4096 | tf_op jit(solution)/shard_map/all_to_all | solution.py:35
  37.7 46.3 %all-to-all-start.2 = ((bf16[8,4,8,128]{3,2,1,0:T(8,128)(2,1)}), bf16[8,4,8,128]{3,2,1,0:T(8,128)(2,1)S(1)}, u32[]{:S(2)}, u32[]{:S(2)}) async-start(bf16[8,4,8,128]{3,2,1,0:T(8,128)(2,1)} %bitcast.3), calls=%async_computation.2 | async-start | bytes 131072 | tf_op jit(solution)/shard_map/all_to_all | solution.py:29
  84.6 7.7 %all-to-all-start.3 = ((bf16[8,4,8,128]{3,2,0,1:T(8,128)(2,1)}), bf16[8,4,8,128]{3,2,0,1:T(8,128)(2,1)S(1)}, u32[]{:S(2)}, u32[]{:S(2)}) async-start(bf16[8,4,8,128]{3,2,0,1:T(8,128)(2,1)} %copy.17), calls=%async_computation.3 | async-start | bytes 131072 | tf_op jit(solution)/shard_map/all_to_all | solution.py:28
where the time goes:
time: 93.7 us; the launch traced here: 93.1 us
  blocking collectives  53.7 us (57%)
  local copies, waits for them, and re-layouts  16.6 us (18%)
  starting transfers between devices  10.1 us (11%)
  waiting for transfers between devices  5.72 us (6%)
  other arithmetic  3.83 us (4%)
  matrix products  1.64 us (2%)
  between operations  1.49 us (2%)
    psum x1, blocking collectives, shards(): total_mass = lax.psum(jnp.sum(bin_mass), ('gx', 'gy'))  39.9 us
    all_to_all x1, blocking collectives, shards(): lax.all_to_all(tagging, 'gx', split_axis=1, concat_axis=1, tiled=True)  13.8 us
    scatter x2, local copies, waits for them, and re-layouts, shards(): tagging.at[0, slots].set(goal_weights).at[1, slots]  13.7 us
    all_to_all x1, waiting for transfers between devices, shards(): lax.all_to_all(lax.all_to_all(outgoing, 'gx', split_axis=0, concat_axis=0...  3.6 us
    all_to_all x1, starting transfers between devices, shards(): lax.all_to_all(lax.all_to_all(outgoing, 'gx', split_axis=0, concat_axis=0...  3.54 us
    all_to_all x1, starting transfers between devices, shards(): lax.all_to_all(outgoing, 'gx', split_axis=0, concat_axis=0, tiled=True)  3.35 us
    all_to_all x1, starting transfers between devices, shards(): lax.all_to_all(lax.all_to_all(tagging, 'gx', split_axis=1, concat_axis=1,...  3.22 us
    all_to_all x1, waiting for transfers between devices, shards(): lax.all_to_all(lax.all_to_all(tagging, 'gx', split_axis=1, concat_axis=1,...  2.11 us
  transfers between devices with their start and end apart: 3, of which 2 were waited for; matrix products, arithmetic and copies ran while one was open for 5% of the time, Pallas kernels for 0%

commit v1 on v0

v1 whole, which is shorter than its diff:
```python
import jax
import jax.numpy as jnp
from jax import lax
from jax.experimental import pallas as pl
from jax.experimental.pallas import tpu as pltpu
from jax.sharding import PartitionSpec as P

BINS_DEV = 64
LANES = 128
OFFSET = 3
SUM = 4


def pieces(x):
    hi = x.astype(jnp.bfloat16).astype(jnp.float32)
    rest = x - hi
    mid = rest.astype(jnp.bfloat16).astype(jnp.float32)
    return hi, mid, rest - mid


def pack(devices, capacity, embed_ref, bins_ref, weights_ref, out_ref):
    goals, width = embed_ref.shape
    bins = bins_ref[...]
    weights = weights_ref[...]
    owners = bins // BINS_DEV
    offsets = bins - owners * BINS_DEV
    owner_ids = lax.broadcasted_iota(jnp.int32, (devices, goals), 0)
    member = owner_ids == owners
    earlier = lax.broadcasted_iota(jnp.int32, (goals, goals), 0) < lax.broadcasted_iota(jnp.int32, (goals, goals), 1)
    before = jnp.dot(
        member.astype(jnp.bfloat16), earlier.astype(jnp.bfloat16), preferred_element_type=jnp.float32
    )
    places = jnp.sum(jnp.where(member, before, 0.0), axis=0, keepdims=True).astype(jnp.int32)
    slots = owners * capacity + places
    rows = lax.broadcasted_iota(jnp.int32, (devices * capacity, goals), 0)
    chosen = (rows == slots).astype(jnp.bfloat16)
    up = jnp.transpose(
        jnp.concatenate([weights, offsets.astype(jnp.float32), jnp.zeros((6, goals), jnp.float32)], axis=0)
    )
    weight = up[:, 0:1]
    offset = up[:, 1:2]
    scaled = (weight * embed_ref[...].astype(jnp.float32)).astype(jnp.bfloat16)
    lane = lax.broadcasted_iota(jnp.int32, (goals, LANES), 1)
    hi, mid, lo = pieces(weight)
    tag = jnp.where(lane == 0, hi, jnp.where(lane == 1, mid, jnp.where(lane == 2, lo, 0.0)))
    tag = jnp.where(lane == OFFSET, offset, tag).astype(jnp.bfloat16)
    out_ref[:, :width] = jnp.dot(chosen, scaled, preferred_element_type=jnp.float32).astype(jnp.bfloat16)
    tags = jnp.dot(chosen, tag, preferred_element_type=jnp.float32)
    hi, mid, lo = pieces(jnp.sum(weights, axis=1, keepdims=True))
    lane = lax.broadcasted_iota(jnp.int32, (1, LANES), 1)
    own = jnp.where(lane == SUM, hi, jnp.where(lane == SUM + 1, mid, jnp.where(lane == SUM + 2, lo, 0.0)))
    out_ref[:, width:] = (tags + own).astype(jnp.bfloat16)


def unpack(bins, capacity, in_ref, mean_ref, rarity_ref):
    width = mean_ref.shape[1]
    tags = in_ref[:, width:]
    offsets = tags[:, OFFSET : OFFSET + 1].astype(jnp.int32)
    labels = lax.broadcasted_iota(jnp.int32, (tags.shape[0], BINS_DEV), 1)
    selector = (offsets == labels).astype(jnp.bfloat16)
    over_rows = (((0,), (0,)), ((), ()))
    sums = lax.dot_general(selector, in_ref[:, :width], over_rows, preferred_element_type=jnp.float32)
    masses = lax.dot_general(selector, tags, over_rows, preferred_element_type=jnp.float32)
    mass = masses[:, 0:1] + masses[:, 1:2] + masses[:, 2:3] + 1.0
    mean_ref[...] = sums / mass
    totals = jnp.sum(tags.astype(jnp.float32), axis=0, keepdims=True)
    total = (totals[:, SUM : SUM + 1] + totals[:, SUM + 1 : SUM + 2] + totals[:, SUM + 2 : SUM + 3]) / capacity
    across = jnp.transpose(jnp.broadcast_to(mass, (BINS_DEV, LANES)))[0:1, :]
    rarity_ref[...] = jnp.log(total / bins) - jnp.log(across)


def shards(goal_embed, goal_bins, goal_weights):
    goals, width = goal_embed.shape
    devices = lax.axis_size("gx") * lax.axis_size("gy")
    capacity = max(2, 2 * goals // devices)
    outgoing = pl.pallas_call(
        lambda *refs: pack(devices, capacity, *refs),
        out_shape=jax.ShapeDtypeStruct((devices * capacity, width + LANES), jnp.bfloat16),
        name="pack",
    )(goal_embed, goal_bins.reshape(1, goals), goal_weights.reshape(1, goals))
    arrived = lax.all_to_all(
        outgoing.reshape(devices, capacity, width + LANES), ("gx", "gy"), split_axis=0, concat_axis=0, tiled=True
    )
    bin_mean, rarity = pl.pallas_call(
        lambda *refs: unpack(BINS_DEV * devices, capacity, *refs),
        out_shape=(
            jax.ShapeDtypeStruct((BINS_DEV, width), jnp.float32),
            jax.ShapeDtypeStruct((1, BINS_DEV), jnp.float32),
        ),
        name="unpack",
    )(arrived.reshape(devices * capacity, width + LANES))
    return bin_mean, rarity.reshape(BINS_DEV)


def solution(mesh):
    in_specs = (P(("gx", "gy"), None), P(("gx", "gy")), P(("gx", "gy")))
    out_specs = (P(("gx", "gy"), None), P(("gx", "gy")))
    return jax.shard_map(shards, mesh=mesh, in_specs=in_specs, out_specs=out_specs, check_vma=False)
```

time: 93.7 us -> 20.3 us (0.22)
  blocking collectives: 53.7 us -> 15.6 us
  local copies, waits for them, and re-layouts: 16.6 us -> 0 us
  starting transfers between devices: 10.1 us -> 0 us
  waiting for transfers between devices: 5.72 us -> 0 us
  other arithmetic: 3.83 us -> 0 us
  Pallas kernels: 0 us -> 3.77 us
  matrix products: 1.64 us -> 0 us
    psum x1 -> x0, blocking collectives: 39.9 us -> none  [shards(): total_mass = lax.psum(jnp.sum(bin_mass), ('gx', 'gy'))]
    scatter x2 -> x0, local copies, waits for them, and re-layouts: 13.7 us -> none  [shards(): tagging.at[0, slots].set(goal_weights).at[1, slots]]
    all_to_all x3 -> x0, starting transfers between devices: 10.1 us -> none  [the longest x1 3.54 us: shards(): lax.all_to_all(lax.all_to_all(outgoing, 'gx', split_axis=0, concat_axis=0...]
    all_to_all x3 -> x0, waiting for transfers between devices: 5.72 us -> none  [the longest x1 3.6 us: shards(): lax.all_to_all(lax.all_to_all(outgoing, 'gx', split_axis=0, concat_axis=0...]
    pallas_call x0 -> x2, Pallas kernels: none -> 3.77 us  [the longest x1 1.95 us: shards(): pl.pallas_call(lambda *refs: unpack(BINS_DEV * devices, capacity, *refs),...]
    all_to_all x1, blocking collectives: 13.8 us -> 15.6 us  [shards(): lax.all_to_all(outgoing.reshape(devices, capacity, width + LANES), ('gx',...]
    dot_general x2 -> x0, matrix products: 1.64 us -> none  [the longest x1 0.83 us: shards(): jnp.dot(selector.astype(jnp.float32), tag_rows[0], precision=lax.Precisio...]
    scatter x1 -> x0, other arithmetic: 1.54 us -> none  [shards(): jnp.zeros((devices * capacity, width), jnp.bfloat16).at[slots].set(scaled)]
  transfers between devices with their start and end apart: 3 -> 0, of which waited for: 2 -> 0; matrix products, arithmetic and copies ran while one was open for 5% -> 0% of each run, Pallas kernels for 0% -> 0%
where the time goes in v1:
time: 20.3 us; the launch traced here: 20 us
  blocking collectives  15.6 us (77%)
  Pallas kernels  3.77 us (19%)
  between operations  0.63 us (3%)
    all_to_all x1, blocking collectives, shards(): lax.all_to_all(outgoing.reshape(devices, capacity, width + LANES), ('gx',...  15.6 us
    pallas_call x1, Pallas kernels, shards(): pl.pallas_call(lambda *refs: unpack(BINS_DEV * devices, capacity, *refs),...  1.95 us
    pallas_call x1, Pallas kernels, shards(): pl.pallas_call(lambda *refs: pack(devices, capacity, *refs), out_shape=ja...  1.82 us

profile of v1, /device:TPU:0, one launch (start us, length us, event | category | flops | bytes accessed | tf_op | source)
XLA Modules:
  0.0 20.0 jit_solution(6136996088918031170)
XLA Ops:
  0.6 1.8 %pack.1 = bf16[256,256]{1,0:T(8,128)(2,1)} custom-call(bf16[128,128]{1,0:T(8,128)(2,1)} %refs_0_.1, s32[1,128]{1,0:T(1,128)} %bitcast.7, f32[1,128]{1,0:T(1,128)} %bitcast.8), custom_call_target="tpu_custom_call" | custom-call | tf_op jit(solution)/shard_map/pack/pallas_call | solution.py:76
  2.4 15.6 %all_to_all.5 = bf16[32,8,256]{2,1,0:T(8,128)(2,1)} all-to-all(bf16[32,8,256]{2,1,0:T(8,128)(2,1)} %bitcast.5), channel_id=1, replica_groups=mesh['gx'=8,'gy'=4] {'gx','gy'}, dimensions={0} | all-to-all | bytes 262144 | tf_op jit(solution)/shard_map/all_to_all | solution.py:81
  18.1 1.9 %unpack.1 = (f32[64,128]{1,0:T(8,128)}, f32[1,64]{1,0:T(1,128)}) custom-call(bf16[256,256]{1,0:T(8,128)(2,1)} %bitcast.6), custom_call_target="tpu_custom_call" | custom-call | tf_op jit(solution)/shard_map/unpack/pallas_call | solution.py:84

commit v2 on v1

--- a/solution.py
+++ b/solution.py
@@ -7,6 +7,7 @@
 
 BINS_DEV = 64
 LANES = 128
+VMEM_BYTES = 4 * 1024 * 1024
 OFFSET = 3
 SUM = 4
 
@@ -18,8 +19,18 @@
     return hi, mid, rest - mid
 
 
-def pack(devices, capacity, embed_ref, bins_ref, weights_ref, out_ref):
+def pack(devices, capacity, embed_hbm, bins_hbm, weights_hbm, out_ref, embed_ref, bins_ref, weights_ref, arrivals):
     goals, width = embed_ref.shape
+    copies = [
+        pltpu.make_async_copy(source, target, arrivals.at[i])
+        for i, (source, target) in enumerate(
+            ((bins_hbm, bins_ref), (weights_hbm, weights_ref), (embed_hbm, embed_ref))
+        )
+    ]
+    for copy in copies:
+        copy.start()
+    for copy in copies:
+        copy.wait()
     bins = bins_ref[...]
     weights = weights_ref[...]
     owners = bins // BINS_DEV
@@ -73,11 +84,20 @@
     goals, width = goal_embed.shape
     devices = lax.axis_size("gx") * lax.axis_size("gy")
     capacity = max(2, 2 * goals // devices)
+    inputs = (goal_embed, goal_bins.reshape(1, goals), goal_weights.reshape(1, goals))
     outgoing = pl.pallas_call(
         lambda *refs: pack(devices, capacity, *refs),
         out_shape=jax.ShapeDtypeStruct((devices * capacity, width + LANES), jnp.bfloat16),
+        in_specs=[pl.BlockSpec(memory_space=pltpu.HBM)] * 3,
+        scratch_shapes=[
+            pltpu.VMEM((goals, width), goal_embed.dtype),
+            pltpu.VMEM((1, goals), goal_bins.dtype),
+            pltpu.VMEM((1, goals), goal_weights.dtype),
+            pltpu.SemaphoreType.DMA((3,)),
+        ],
+        compiler_params=pltpu.CompilerParams(vmem_limit_bytes=VMEM_BYTES),
         name="pack",
-    )(goal_embed, goal_bins.reshape(1, goals), goal_weights.reshape(1, goals))
+    )(*(pltpu.with_memory_space_constraint(x, pltpu.HBM) for x in inputs))
     arrived = lax.all_to_all(
         outgoing.reshape(devices, capacity, width + LANES), ("gx", "gy"), split_axis=0, concat_axis=0, tiled=True
     )
@@ -87,6 +107,7 @@
             jax.ShapeDtypeStruct((BINS_DEV, width), jnp.float32),
             jax.ShapeDtypeStruct((1, BINS_DEV), jnp.float32),
         ),
+        compiler_params=pltpu.CompilerParams(vmem_limit_bytes=VMEM_BYTES),
         name="unpack",
     )(arrived.reshape(devices * capacity, width + LANES))
     return bin_mean, rarity.reshape(BINS_DEV)

time: 20.3 us -> 18.4 us (0.906)
  Pallas kernels: 3.77 us -> 2.24 us
  blocking collectives: 15.6 us -> 15.3 us
    pallas_call x1, Pallas kernels: 1.95 us -> 1.04 us  [shards(): pl.pallas_call(lambda *refs: unpack(BINS_DEV * devices, capacity, *refs),...]
    pallas_call x1, Pallas kernels: 1.82 us -> 1.2 us  [shards(): pl.pallas_call(lambda *refs: pack(devices, capacity, *refs), out_shape=ja...]
    all_to_all x1, blocking collectives: 15.6 us -> 15.3 us  [shards(): lax.all_to_all(outgoing.reshape(devices, capacity, width + LANES), ('gx',...]
where the time goes in v2:
time: 18.4 us; the launch traced here: 18.2 us
  blocking collectives  15.3 us (83%)
  Pallas kernels  2.24 us (12%)
  between operations  0.64 us (3%)
    all_to_all x1, blocking collectives, shards(): lax.all_to_all(outgoing.reshape(devices, capacity, width + LANES), ('gx',...  15.3 us
    pallas_call x1, Pallas kernels, shards(): pl.pallas_call(lambda *refs: pack(devices, capacity, *refs), out_shape=ja...  1.2 us
    pallas_call x1, Pallas kernels, shards(): pl.pallas_call(lambda *refs: unpack(BINS_DEV * devices, capacity, *refs),...  1.04 us

profile of v2, /device:TPU:0, one launch (start us, length us, event | category | flops | bytes accessed | tf_op | source)
XLA Modules:
  0.0 18.2 jit_solution(14758714749452457485)
XLA Ops:
  0.6 1.2 %pack.1 = bf16[256,256]{1,0:T(8,128)(2,1)S(1)} custom-call(bf16[128,128]{1,0:T(8,128)(2,1)} %refs_0_.1, s32[1,128]{1,0:T(1,128)} %bitcast.7, f32[1,128]{1,0:T(1,128)} %bitcast.8), custom_call_target="tpu_custom_call" | custom-call | tf_op jit(solution)/shard_map/pack/pallas_call | solution.py:88
  1.8 15.3 %all_to_all.5 = bf16[32,8,256]{2,1,0:T(8,128)(2,1)S(1)} all-to-all(bf16[32,8,256]{2,1,0:T(8,128)(2,1)S(1)} %bitcast.5), channel_id=1, replica_groups=mesh['gx'=8,'gy'=4] {'gx','gy'}, dimensions={0} | all-to-all | bytes 262144 | tf_op jit(solution)/shard_map/all_to_all | solution.py:101
  17.2 1.0 %unpack.1 = (f32[64,128]{1,0:T(8,128)}, f32[1,64]{1,0:T(1,128)}) custom-call(bf16[256,256]{1,0:T(8,128)(2,1)S(1)} %bitcast.6), custom_call_target="tpu_custom_call" | custom-call | tf_op jit(solution)/shard_map/unpack/pallas_call | solution.py:104

commit v3 on v2

v3 whole, which is shorter than its diff:
```python
import jax
import jax.numpy as jnp
from jax import lax
from jax.experimental import pallas as pl
from jax.experimental.pallas import tpu as pltpu
from jax.sharding import PartitionSpec as P

BINS_DEV = 64
LANES = 128
VMEM_BYTES = 4 * 1024 * 1024
OFFSET = 3
SUM = 4


def pieces(x):
    hi = x.astype(jnp.bfloat16).astype(jnp.float32)
    rest = x - hi
    mid = rest.astype(jnp.bfloat16).astype(jnp.float32)
    return hi, mid, rest - mid


def one_hot(mask):
    return jnp.where(mask, 1.0, 0.0).astype(jnp.bfloat16)


def iota(shape, dimension):
    return lax.broadcasted_iota(jnp.int32, shape, dimension)


def pack(devices, capacity, embed_hbm, bins_hbm, weights_hbm, out_ref, embed_ref, bins_ref, weights_ref, arrivals):
    goals = embed_ref.shape[0]
    copies = [
        pltpu.make_async_copy(source, target, arrivals.at[i])
        for i, (source, target) in enumerate(
            ((bins_hbm, bins_ref), (weights_hbm, weights_ref), (embed_hbm, embed_ref))
        )
    ]
    for copy in copies:
        copy.start()
    stride = capacity + 2
    rows = iota((devices * stride, goals), 0)
    for copy in copies:
        copy.wait()
    bins = bins_ref[...]
    weights = weights_ref[...]
    owners = bins // BINS_DEV
    offsets = (bins - owners * BINS_DEV).astype(jnp.float32)
    member = iota((devices, goals), 0) == owners
    earlier = iota((goals, goals), 0) < iota((goals, goals), 1)
    before = jnp.dot(one_hot(member), one_hot(earlier), preferred_element_type=jnp.float32)
    places = jnp.sum(jnp.where(member, before, 0.0), axis=0, keepdims=True).astype(jnp.int32)
    bases = owners * stride
    chosen = one_hot(rows == bases + places)
    up = jnp.transpose(jnp.concatenate([weights, jnp.zeros((7, goals), jnp.float32)], axis=0))
    scaled = (up[:, 0:1] * embed_ref[...].astype(jnp.float32)).astype(jnp.bfloat16)
    tagged = one_hot(rows == bases + capacity)
    hi, mid, lo = pieces(weights)
    lane = iota((LANES, goals), 0)
    tags = jnp.zeros((LANES, goals), jnp.float32)
    for field, value in enumerate((hi, mid, lo, offsets)):
        tags = jnp.where(lane == places + field * capacity, value, tags)
    lane = iota((LANES, devices), 0)
    own = jnp.zeros((LANES, devices), jnp.float32)
    for field, value in enumerate(pieces(jnp.sum(weights, axis=1, keepdims=True))):
        own = jnp.where(lane == SUM * capacity + field, value, own)
    every = one_hot(iota((devices * stride, devices), 0) == iota((devices * stride, devices), 1) * stride + capacity)
    across = (((1,), (1,)), ((), ()))
    out = jnp.dot(chosen, scaled, preferred_element_type=jnp.float32)
    out += lax.dot_general(tagged, tags.astype(jnp.bfloat16), across, preferred_element_type=jnp.float32)
    out += lax.dot_general(every, own.astype(jnp.bfloat16), across, preferred_element_type=jnp.float32)
    out_ref[...] = out.astype(jnp.bfloat16)


def unpack(devices, capacity, in_ref, mean_ref, rarity_ref):
    stride = capacity + 2
    slots = devices * stride
    arrived = in_ref[...]
    tag_rows = one_hot(iota((devices, slots), 1) == iota((devices, slots), 0) * stride + capacity)
    tags = jnp.dot(tag_rows, arrived, preferred_element_type=jnp.float32)
    slot = iota((LANES, slots), 1)
    place = slot - ((slot.astype(jnp.float32) + 0.5) * (1.0 / stride)).astype(jnp.int32) * stride
    lane = iota((LANES, slots), 0)
    pick = one_hot(lane == place + OFFSET * capacity)
    gather = one_hot((lane == place) | (lane == place + capacity) | (lane == place + 2 * capacity))
    first = iota((devices, slots), 1) - iota((devices, slots), 0) * stride
    here = (first >= 0) & (first < capacity)
    tags = tags.astype(jnp.bfloat16)
    offsets = jnp.dot(tags, pick, preferred_element_type=jnp.float32)
    weights = jnp.dot(tags, gather, preferred_element_type=jnp.float32)
    offsets = jnp.sum(jnp.where(here, offsets + 1.0, 0.0), axis=0, keepdims=True)
    weights = jnp.sum(jnp.where(here, weights, 0.0), axis=0, keepdims=True)
    selector = iota((BINS_DEV, slots), 0) + 1 == offsets.astype(jnp.int32)
    sums = jnp.dot(one_hot(selector), arrived, preferred_element_type=jnp.float32)
    mass = jnp.sum(jnp.where(selector, weights, 0.0), axis=1, keepdims=True) + 1.0
    mean_ref[...] = sums / mass
    totals = jnp.sum(tags.astype(jnp.float32), axis=0, keepdims=True)
    lane = iota(totals.shape, 1)
    own = (lane >= SUM * capacity) & (lane < SUM * capacity + 3)
    total = jnp.sum(jnp.where(own, totals, 0.0), axis=1, keepdims=True)
    across = jnp.transpose(jnp.broadcast_to(mass, (BINS_DEV, LANES)))[0:1, :]
    rarity_ref[...] = jnp.log(total / (BINS_DEV * devices)) - jnp.log(across)


def shards(goal_embed, goal_bins, goal_weights):
    goals, width = goal_embed.shape
    devices = lax.axis_size("gx") * lax.axis_size("gy")
    capacity = max(2, 2 * goals // devices)
    capacity += capacity % 2
    stride = capacity + 2
    inputs = (goal_embed, goal_bins.reshape(1, goals), goal_weights.reshape(1, goals))
    outgoing = pl.pallas_call(
        lambda *refs: pack(devices, capacity, *refs),
        out_shape=jax.ShapeDtypeStruct((devices * stride, width), jnp.bfloat16),
        in_specs=[pl.BlockSpec(memory_space=pltpu.HBM)] * 3,
        scratch_shapes=[
            pltpu.VMEM((goals, width), goal_embed.dtype),
            pltpu.VMEM((1, goals), goal_bins.dtype),
            pltpu.VMEM((1, goals), goal_weights.dtype),
            pltpu.SemaphoreType.DMA((3,)),
        ],
        compiler_params=pltpu.CompilerParams(vmem_limit_bytes=VMEM_BYTES),
        name="pack",
    )(*(pltpu.with_memory_space_constraint(x, pltpu.HBM) for x in inputs))
    arrived = lax.all_to_all(
        outgoing.reshape(devices, stride // 2, 2, width), ("gx", "gy"), split_axis=0, concat_axis=0, tiled=True
    )
    bin_mean, rarity = pl.pallas_call(
        lambda *refs: unpack(devices, capacity, *refs),
        out_shape=(
            jax.ShapeDtypeStruct((BINS_DEV, width), jnp.float32),
            jax.ShapeDtypeStruct((1, BINS_DEV), jnp.float32),
        ),
        compiler_params=pltpu.CompilerParams(vmem_limit_bytes=VMEM_BYTES),
        name="unpack",
    )(arrived.reshape(devices * stride, width))
    return bin_mean, rarity.reshape(BINS_DEV)


def solution(mesh):
    in_specs = (P(("gx", "gy"), None), P(("gx", "gy")), P(("gx", "gy")))
    out_specs = (P(("gx", "gy"), None), P(("gx", "gy")))
    return jax.shard_map(shards, mesh=mesh, in_specs=in_specs, out_specs=out_specs, check_vma=False)
```

time: 18.4 us -> 17.8 us (0.967)
  blocking collectives: 15.3 us -> 14.7 us
    all_to_all x1, blocking collectives: 15.3 us -> 14.7 us  [shards(): lax.all_to_all(outgoing.reshape(devices, stride // 2, 2, width), ('gx', '...]
where the time goes in v3:
time: 17.8 us; the launch traced here: 17.6 us
  blocking collectives  14.7 us (83%)
  Pallas kernels  2.23 us (13%)
  between operations  0.64 us (4%)
    all_to_all x1, blocking collectives, shards(): lax.all_to_all(outgoing.reshape(devices, stride // 2, 2, width), ('gx', '...  14.7 us
    pallas_call x1, Pallas kernels, shards(): pl.pallas_call(lambda *refs: pack(devices, capacity, *refs), out_shape=ja...  1.2 us
    pallas_call x1, Pallas kernels, shards(): pl.pallas_call(lambda *refs: unpack(devices, capacity, *refs), out_shape=...  1.03 us

profile of v3, /device:TPU:0, one launch (start us, length us, event | category | flops | bytes accessed | tf_op | source)
XLA Modules:
  0.0 17.6 jit_solution(17000024133530794214)
XLA Ops:
  0.6 1.2 %pack.1 = bf16[320,128]{1,0:T(8,128)(2,1)S(1)} custom-call(bf16[128,128]{1,0:T(8,128)(2,1)} %refs_0_.1, s32[1,128]{1,0:T(1,128)} %bitcast.7, f32[1,128]{1,0:T(1,128)} %bitcast.8), custom_call_target="tpu_custom_call" | custom-call | tf_op jit(solution)/shard_map/pack/pallas_call | solution.py:111
  1.8 14.7 %all_to_all.5 = bf16[32,5,2,128]{3,2,1,0:T(2,128)(2,1)S(1)} all-to-all(bf16[32,5,2,128]{3,2,1,0:T(2,128)(2,1)S(1)} %bitcast.6), channel_id=1, replica_groups=mesh['gx'=8,'gy'=4] {'gx','gy'}, dimensions={0} | all-to-all | bytes 163840 | tf_op jit(solution)/shard_map/all_to_all | solution.py:124
  16.6 1.0 %unpack.1 = (f32[64,128]{1,0:T(8,128)}, f32[1,64]{1,0:T(1,128)}) custom-call(bf16[320,128]{1,0:T(8,128)(2,1)S(1)} %bitcast.5), custom_call_target="tpu_custom_call" | custom-call | tf_op jit(solution)/shard_map/unpack/pallas_call | solution.py:127

commit v4 on v3

v4 whole, which is shorter than its diff:
```python
import jax
import jax.numpy as jnp
from jax import lax
from jax.experimental import pallas as pl
from jax.experimental.pallas import tpu as pltpu
from jax.sharding import PartitionSpec as P

BINS_DEV = 64
LANES = 128
VMEM_BYTES = 4 * 1024 * 1024
FIELD = LANES // 4


def pieces(x):
    hi = x.astype(jnp.bfloat16).astype(jnp.float32)
    rest = x - hi
    mid = rest.astype(jnp.bfloat16).astype(jnp.float32)
    return hi, mid, rest - mid


def one_hot(mask):
    return jnp.where(mask, 1.0, 0.0).astype(jnp.bfloat16)


def iota(shape, dimension):
    return lax.broadcasted_iota(jnp.int32, shape, dimension)


def pack(devices, capacity, embed_hbm, bins_hbm, weights_hbm, out_ref, embed_ref, bins_ref, weights_ref, stage_ref, arrivals):
    goals = embed_ref.shape[0]
    copies = [
        pltpu.make_async_copy(source, target, arrivals.at[i])
        for i, (source, target) in enumerate(
            ((bins_hbm, bins_ref), (weights_hbm, weights_ref), (embed_hbm, embed_ref))
        )
    ]
    for copy in copies:
        copy.start()
    stride = capacity + 2
    rows = iota((devices * stride, goals), 0)
    for copy in copies:
        copy.wait()
    bins = bins_ref[...]
    weights = weights_ref[...]
    owners = bins // BINS_DEV
    offsets = (bins - owners * BINS_DEV).astype(jnp.float32)
    member = iota((devices, goals), 0) == owners
    earlier = iota((goals, goals), 0) < iota((goals, goals), 1)
    before = jnp.dot(one_hot(member), one_hot(earlier), preferred_element_type=jnp.float32)
    places = jnp.sum(jnp.where(member, before, 0.0), axis=0, keepdims=True).astype(jnp.int32)
    chosen = one_hot(rows == owners * stride + places)
    up = jnp.transpose(jnp.concatenate([weights, jnp.zeros((7, goals), jnp.float32)], axis=0))
    scaled = (up[:, 0:1] * embed_ref[...].astype(jnp.float32)).astype(jnp.bfloat16)
    me = lax.axis_index("gx") * lax.axis_size("gy") + lax.axis_index("gy")
    lane = lax.rem(iota((LANES, goals), 0) + (LANES - lax.rem(me * stride, LANES)), LANES)
    tags = jnp.zeros((LANES, goals), jnp.float32)
    for field, value in enumerate((offsets, *pieces(weights))):
        tags = jnp.where(lane == places + field * FIELD, value, tags)
    across = (((1,), (1,)), ((), ()))
    tags = lax.dot_general(
        one_hot(member), tags.astype(jnp.bfloat16), across, preferred_element_type=jnp.float32
    )
    lane = lax.rem(iota(tags.shape, 1) + (LANES - lax.rem(me * stride, LANES)), LANES)
    for i, piece in enumerate(pieces(jnp.sum(weights, axis=1, keepdims=True))):
        tags = jnp.where(lane == capacity + i, piece, tags)
    stage_ref[...] = jnp.dot(chosen, scaled, preferred_element_type=jnp.float32)
    stage_ref[pl.ds(capacity, devices, stride=stride), :] = tags
    out_ref[...] = stage_ref[...].astype(jnp.bfloat16)


def unpack(devices, capacity, in_ref, mean_ref, rarity_ref, stage_ref):
    stride = capacity + 2
    slots = devices * stride
    stage_ref[...] = in_ref[...].astype(jnp.float32)
    tags = stage_ref[pl.ds(capacity, devices, stride=stride), :]
    fields = [tags, *(pltpu.roll(tags, LANES - field * FIELD, 1) for field in range(1, 4))]
    tiles = pl.cdiv(slots, LANES)
    place = iota((devices, tiles * LANES), 1) - iota((devices, tiles * LANES), 0) * stride
    here = (place >= 0) & (place < capacity)

    def spread(x):
        return jnp.sum(jnp.where(here, jnp.concatenate([x] * tiles, axis=1), 0.0), axis=0, keepdims=True)

    offsets = spread(fields[0] + 1.0)
    weights = spread(fields[1] + fields[2] + fields[3])
    selector = iota((BINS_DEV, tiles * LANES), 0) + 1 == offsets.astype(jnp.int32)
    chosen = one_hot(selector)
    sums = jnp.dot(chosen[:, :slots], in_ref[...], preferred_element_type=jnp.float32)
    mass = jnp.sum(jnp.where(selector, weights, 0.0), axis=1, keepdims=True) + 1.0
    mean_ref[...] = sums / mass
    turned = LANES - lax.rem(iota(tags.shape, 0) * stride, LANES)
    lane = lax.rem(iota(tags.shape, 1) + turned, LANES)
    own = (lane >= capacity) & (lane < capacity + 3)
    total = jnp.sum(jnp.sum(jnp.where(own, tags, 0.0), axis=0, keepdims=True), axis=1, keepdims=True)
    parts = jnp.concatenate([*pieces(weights), jnp.zeros((5, tiles * LANES), jnp.float32)], axis=0)
    across = (((1,), (1,)), ((), ()))
    masses = lax.dot_general(parts.astype(jnp.bfloat16), chosen, across, preferred_element_type=jnp.float32)
    masses = jnp.sum(masses, axis=0, keepdims=True) + 1.0
    rarity_ref[...] = jnp.log(total / (BINS_DEV * devices)) - jnp.log(masses)


def shards(goal_embed, goal_bins, goal_weights):
    goals, width = goal_embed.shape
    devices = lax.axis_size("gx") * lax.axis_size("gy")
    capacity = max(2, 2 * goals // devices)
    capacity += capacity % 2
    stride = capacity + 2
    inputs = (goal_embed, goal_bins.reshape(1, goals), goal_weights.reshape(1, goals))
    outgoing = pl.pallas_call(
        lambda *refs: pack(devices, capacity, *refs),
        out_shape=jax.ShapeDtypeStruct((devices * stride, width), jnp.bfloat16),
        in_specs=[pl.BlockSpec(memory_space=pltpu.HBM)] * 3,
        scratch_shapes=[
            pltpu.VMEM((goals, width), goal_embed.dtype),
            pltpu.VMEM((1, goals), goal_bins.dtype),
            pltpu.VMEM((1, goals), goal_weights.dtype),
            pltpu.VMEM((devices * stride, width), jnp.float32),
            pltpu.SemaphoreType.DMA((3,)),
        ],
        compiler_params=pltpu.CompilerParams(vmem_limit_bytes=VMEM_BYTES),
        name="pack",
    )(*(pltpu.with_memory_space_constraint(x, pltpu.HBM) for x in inputs))
    arrived = lax.all_to_all(
        outgoing.reshape(devices, stride // 2, 2, width), ("gx", "gy"), split_axis=0, concat_axis=0, tiled=True
    )
    bin_mean, rarity = pl.pallas_call(
        lambda *refs: unpack(devices, capacity, *refs),
        out_shape=(
            jax.ShapeDtypeStruct((BINS_DEV, width), jnp.float32),
            jax.ShapeDtypeStruct((1, BINS_DEV), jnp.float32),
        ),
        scratch_shapes=[pltpu.VMEM((devices * stride, width), jnp.float32)],
        compiler_params=pltpu.CompilerParams(vmem_limit_bytes=VMEM_BYTES),
        name="unpack",
    )(arrived.reshape(devices * stride, width))
    return bin_mean, rarity.reshape(BINS_DEV)


def solution(mesh):
    in_specs = (P(("gx", "gy"), None), P(("gx", "gy")), P(("gx", "gy")))
    out_specs = (P(("gx", "gy"), None), P(("gx", "gy")))
    return jax.shard_map(shards, mesh=mesh, in_specs=in_specs, out_specs=out_specs, check_vma=False)
```

time: 17.8 us -> 17.5 us (0.983)
  Pallas kernels: 2.23 us -> 1.97 us
    pallas_call x1, Pallas kernels: 1.03 us -> 0.81 us  [shards(): pl.pallas_call(lambda *refs: unpack(devices, capacity, *refs), out_shape=...]
where the time goes in v4:
time: 17.5 us; the launch traced here: 17.3 us
  blocking collectives  14.7 us (84%)
  Pallas kernels  1.97 us (11%)
  between operations  0.64 us (4%)
    all_to_all x1, blocking collectives, shards(): lax.all_to_all(outgoing.reshape(devices, stride // 2, 2, width), ('gx', '...  14.7 us
    pallas_call x1, Pallas kernels, shards(): pl.pallas_call(lambda *refs: pack(devices, capacity, *refs), out_shape=ja...  1.16 us
    pallas_call x1, Pallas kernels, shards(): pl.pallas_call(lambda *refs: unpack(devices, capacity, *refs), out_shape=...  0.81 us

profile of v4, /device:TPU:0, one launch (start us, length us, event | category | flops | bytes accessed | tf_op | source)
XLA Modules:
  0.0 17.3 jit_solution(9271806516816466533)
XLA Ops:
  0.6 1.2 %pack.1 = bf16[320,128]{1,0:T(8,128)(2,1)S(1)} custom-call(bf16[128,128]{1,0:T(8,128)(2,1)} %refs_0_.1, s32[1,128]{1,0:T(1,128)} %bitcast.7, f32[1,128]{1,0:T(1,128)} %bitcast.8), custom_call_target="tpu_custom_call" | custom-call | tf_op jit(solution)/shard_map/pack/pallas_call | solution.py:109
  1.8 14.7 %all_to_all.5 = bf16[32,5,2,128]{3,2,1,0:T(2,128)(2,1)S(1)} all-to-all(bf16[32,5,2,128]{3,2,1,0:T(2,128)(2,1)S(1)} %bitcast.6), channel_id=1, replica_groups=mesh['gx'=8,'gy'=4] {'gx','gy'}, dimensions={0} | all-to-all | bytes 163840 | tf_op jit(solution)/shard_map/all_to_all | solution.py:123
  16.5 0.8 %unpack.1 = (f32[64,128]{1,0:T(8,128)}, f32[1,64]{1,0:T(1,128)}) custom-call(bf16[320,128]{1,0:T(8,128)(2,1)S(1)} %bitcast.5), custom_call_target="tpu_custom_call" | custom-call | tf_op jit(solution)/shard_map/unpack/pallas_call | solution.py:126

commit v5 on v4

--- a/solution.py
+++ b/solution.py
@@ -22,12 +22,18 @@
     return jnp.where(mask, 1.0, 0.0).astype(jnp.bfloat16)
 
 
+def quotient(x, n):
+    return x >> (n.bit_length() - 1) if n & (n - 1) == 0 else lax.div(x, n)
+
+
 def iota(shape, dimension):
     return lax.broadcasted_iota(jnp.int32, shape, dimension)
 
 
-def pack(devices, capacity, embed_hbm, bins_hbm, weights_hbm, out_ref, embed_ref, bins_ref, weights_ref, stage_ref, arrivals):
+def pack(capacity, embed_hbm, bins_hbm, weights_hbm, out_ref, embed_ref, bins_ref, weights_ref, stage_ref, arrivals):
     goals = embed_ref.shape[0]
+    across, along = lax.axis_size("gx"), lax.axis_size("gy")
+    devices = across * along
     copies = [
         pltpu.make_async_copy(source, target, arrivals.at[i])
         for i, (source, target) in enumerate(
@@ -42,8 +48,10 @@
         copy.wait()
     bins = bins_ref[...]
     weights = weights_ref[...]
-    owners = bins // BINS_DEV
+    owners = quotient(bins, BINS_DEV)
     offsets = (bins - owners * BINS_DEV).astype(jnp.float32)
+    major = quotient(owners, along)
+    owners = (owners - major * along) * across + major
     member = iota((devices, goals), 0) == owners
     earlier = iota((goals, goals), 0) < iota((goals, goals), 1)
     before = jnp.dot(one_hot(member), one_hot(earlier), preferred_element_type=jnp.float32)
@@ -51,14 +59,14 @@
     chosen = one_hot(rows == owners * stride + places)
     up = jnp.transpose(jnp.concatenate([weights, jnp.zeros((7, goals), jnp.float32)], axis=0))
     scaled = (up[:, 0:1] * embed_ref[...].astype(jnp.float32)).astype(jnp.bfloat16)
-    me = lax.axis_index("gx") * lax.axis_size("gy") + lax.axis_index("gy")
+    me = lax.axis_index("gy") * across + lax.axis_index("gx")
     lane = lax.rem(iota((LANES, goals), 0) + (LANES - lax.rem(me * stride, LANES)), LANES)
     tags = jnp.zeros((LANES, goals), jnp.float32)
     for field, value in enumerate((offsets, *pieces(weights))):
         tags = jnp.where(lane == places + field * FIELD, value, tags)
-    across = (((1,), (1,)), ((), ()))
+    over_lanes = (((1,), (1,)), ((), ()))
     tags = lax.dot_general(
-        one_hot(member), tags.astype(jnp.bfloat16), across, preferred_element_type=jnp.float32
+        one_hot(member), tags.astype(jnp.bfloat16), over_lanes, preferred_element_type=jnp.float32
     )
     lane = lax.rem(iota(tags.shape, 1) + (LANES - lax.rem(me * stride, LANES)), LANES)
     for i, piece in enumerate(pieces(jnp.sum(weights, axis=1, keepdims=True))):
@@ -93,8 +101,8 @@
     own = (lane >= capacity) & (lane < capacity + 3)
     total = jnp.sum(jnp.sum(jnp.where(own, tags, 0.0), axis=0, keepdims=True), axis=1, keepdims=True)
     parts = jnp.concatenate([*pieces(weights), jnp.zeros((5, tiles * LANES), jnp.float32)], axis=0)
-    across = (((1,), (1,)), ((), ()))
-    masses = lax.dot_general(parts.astype(jnp.bfloat16), chosen, across, preferred_element_type=jnp.float32)
+    over_lanes = (((1,), (1,)), ((), ()))
+    masses = lax.dot_general(parts.astype(jnp.bfloat16), chosen, over_lanes, preferred_element_type=jnp.float32)
     masses = jnp.sum(masses, axis=0, keepdims=True) + 1.0
     rarity_ref[...] = jnp.log(total / (BINS_DEV * devices)) - jnp.log(masses)
 
@@ -107,7 +115,7 @@
     stride = capacity + 2
     inputs = (goal_embed, goal_bins.reshape(1, goals), goal_weights.reshape(1, goals))
     outgoing = pl.pallas_call(
-        lambda *refs: pack(devices, capacity, *refs),
+        lambda *refs: pack(capacity, *refs),
         out_shape=jax.ShapeDtypeStruct((devices * stride, width), jnp.bfloat16),
         in_specs=[pl.BlockSpec(memory_space=pltpu.HBM)] * 3,
         scratch_shapes=[
@@ -121,7 +129,7 @@
         name="pack",
     )(*(pltpu.with_memory_space_constraint(x, pltpu.HBM) for x in inputs))
     arrived = lax.all_to_all(
-        outgoing.reshape(devices, stride // 2, 2, width), ("gx", "gy"), split_axis=0, concat_axis=0, tiled=True
+        outgoing.reshape(devices, stride // 2, 2, width), ("gy", "gx"), split_axis=0, concat_axis=0, tiled=True
     )
     bin_mean, rarity = pl.pallas_call(
         lambda *refs: unpack(devices, capacity, *refs),

time: 17.5 us -> 17.4 us (level)
  blocking collectives: 14.7 us -> 14.5 us
where the time goes in v5:
time: 17.4 us; the launch traced here: 17.2 us
  blocking collectives  14.5 us (83%)
  Pallas kernels  1.97 us (11%)
  between operations  0.64 us (4%)
    all_to_all x1, blocking collectives, shards(): lax.all_to_all(outgoing.reshape(devices, stride // 2, 2, width), ('gy', '...  14.5 us
    pallas_call x1, Pallas kernels, shards(): pl.pallas_call(lambda *refs: pack(capacity, *refs), out_shape=jax.ShapeDt...  1.16 us
    pallas_call x1, Pallas kernels, shards(): pl.pallas_call(lambda *refs: unpack(devices, capacity, *refs), out_shape=...  0.81 us

profile of v5, /device:TPU:0, one launch (start us, length us, event | category | flops | bytes accessed | tf_op | source)
XLA Modules:
  0.0 17.2 jit_solution(9537409213054495491)
XLA Ops:
  0.6 1.2 %pack.1 = bf16[320,128]{1,0:T(8,128)(2,1)S(1)} custom-call(bf16[128,128]{1,0:T(8,128)(2,1)} %refs_0_.1, s32[1,128]{1,0:T(1,128)} %bitcast.7, f32[1,128]{1,0:T(1,128)} %bitcast.8), custom_call_target="tpu_custom_call" | custom-call | tf_op jit(solution)/shard_map/pack/pallas_call | solution.py:117
  1.8 14.5 %all_to_all.5 = bf16[32,5,2,128]{3,2,1,0:T(2,128)(2,1)S(1)} all-to-all(bf16[32,5,2,128]{3,2,1,0:T(2,128)(2,1)S(1)} %bitcast.6), channel_id=1, replica_groups=mesh['gx'=8,'gy'=4] {'gy','gx'}, dimensions={0} | all-to-all | bytes 163840 | tf_op jit(solution)/shard_map/all_to_all | solution.py:131
  16.3 0.8 %unpack.1 = (f32[64,128]{1,0:T(8,128)}, f32[1,64]{1,0:T(1,128)}) custom-call(bf16[320,128]{1,0:T(8,128)(2,1)S(1)} %bitcast.5), custom_call_target="tpu_custom_call" | custom-call | tf_op jit(solution)/shard_map/unpack/pallas_call | solution.py:134

commit v6 on v5

--- a/solution.py
+++ b/solution.py
@@ -44,7 +44,7 @@
         copy.start()
     stride = capacity + 2
     rows = iota((devices * stride, goals), 0)
-    for copy in copies:
+    for copy in copies[:2]:
         copy.wait()
     bins = bins_ref[...]
     weights = weights_ref[...]
@@ -58,20 +58,25 @@
     places = jnp.sum(jnp.where(member, before, 0.0), axis=0, keepdims=True).astype(jnp.int32)
     chosen = one_hot(rows == owners * stride + places)
     up = jnp.transpose(jnp.concatenate([weights, jnp.zeros((7, goals), jnp.float32)], axis=0))
+    copies[2].wait()
     scaled = (up[:, 0:1] * embed_ref[...].astype(jnp.float32)).astype(jnp.bfloat16)
     me = lax.axis_index("gy") * across + lax.axis_index("gx")
-    lane = lax.rem(iota((LANES, goals), 0) + (LANES - lax.rem(me * stride, LANES)), LANES)
-    tags = jnp.zeros((LANES, goals), jnp.float32)
-    for field, value in enumerate((offsets, *pieces(weights))):
-        tags = jnp.where(lane == places + field * FIELD, value, tags)
+    tall = pl.cdiv(capacity, 8) * 8
+    place = iota((tall, goals), 0) == places
+    blank = jnp.zeros((FIELD - tall, goals), jnp.float32)
+    tags = []
+    for value in (offsets, *pieces(weights)):
+        tags += [jnp.where(place, value, 0.0), blank]
+    tags = jnp.concatenate(tags, axis=0)
     over_lanes = (((1,), (1,)), ((), ()))
     tags = lax.dot_general(
         one_hot(member), tags.astype(jnp.bfloat16), over_lanes, preferred_element_type=jnp.float32
     )
-    lane = lax.rem(iota(tags.shape, 1) + (LANES - lax.rem(me * stride, LANES)), LANES)
+    lane = iota(tags.shape, 1)
     for i, piece in enumerate(pieces(jnp.sum(weights, axis=1, keepdims=True))):
         tags = jnp.where(lane == capacity + i, piece, tags)
     stage_ref[...] = jnp.dot(chosen, scaled, preferred_element_type=jnp.float32)
+    tags = pltpu.roll(tags, (me * stride) & (LANES - 1), 1)
     stage_ref[pl.ds(capacity, devices, stride=stride), :] = tags
     out_ref[...] = stage_ref[...].astype(jnp.bfloat16)
 
@@ -96,8 +101,7 @@
     sums = jnp.dot(chosen[:, :slots], in_ref[...], preferred_element_type=jnp.float32)
     mass = jnp.sum(jnp.where(selector, weights, 0.0), axis=1, keepdims=True) + 1.0
     mean_ref[...] = sums / mass
-    turned = LANES - lax.rem(iota(tags.shape, 0) * stride, LANES)
-    lane = lax.rem(iota(tags.shape, 1) + turned, LANES)
+    lane = (iota(tags.shape, 1) - iota(tags.shape, 0) * stride) & (LANES - 1)
     own = (lane >= capacity) & (lane < capacity + 3)
     total = jnp.sum(jnp.sum(jnp.where(own, tags, 0.0), axis=0, keepdims=True), axis=1, keepdims=True)
     parts = jnp.concatenate([*pieces(weights), jnp.zeros((5, tiles * LANES), jnp.float32)], axis=0)

time: 17.4 us -> 17.3 us (level)
  no operation moved by 1% of the time
where the time goes in v6:
time: 17.3 us; the launch traced here: 17.1 us
  blocking collectives  14.5 us (84%)
  Pallas kernels  1.93 us (11%)
  between operations  0.64 us (4%)
    all_to_all x1, blocking collectives, shards(): lax.all_to_all(outgoing.reshape(devices, stride // 2, 2, width), ('gy', '...  14.5 us
    pallas_call x1, Pallas kernels, shards(): pl.pallas_call(lambda *refs: pack(capacity, *refs), out_shape=jax.ShapeDt...  1.12 us
    pallas_call x1, Pallas kernels, shards(): pl.pallas_call(lambda *refs: unpack(devices, capacity, *refs), out_shape=...  0.81 us

profile of v6, /device:TPU:0, one launch (start us, length us, event | category | flops | bytes accessed | tf_op | source)
XLA Modules:
  0.0 17.1 jit_solution(4885364846009634328)
XLA Ops:
  0.6 1.1 %pack.1 = bf16[320,128]{1,0:T(8,128)(2,1)S(1)} custom-call(bf16[128,128]{1,0:T(8,128)(2,1)} %refs_0_.1, s32[1,128]{1,0:T(1,128)} %bitcast.7, f32[1,128]{1,0:T(1,128)} %bitcast.8), custom_call_target="tpu_custom_call" | custom-call | tf_op jit(solution)/shard_map/pack/pallas_call | solution.py:121
  1.8 14.5 %all_to_all.5 = bf16[32,5,2,128]{3,2,1,0:T(2,128)(2,1)S(1)} all-to-all(bf16[32,5,2,128]{3,2,1,0:T(2,128)(2,1)S(1)} %bitcast.6), channel_id=1, replica_groups=mesh['gx'=8,'gy'=4] {'gy','gx'}, dimensions={0} | all-to-all | bytes 163840 | tf_op jit(solution)/shard_map/all_to_all | solution.py:135
  16.3 0.8 %unpack.1 = (f32[64,128]{1,0:T(8,128)}, f32[1,64]{1,0:T(1,128)}) custom-call(bf16[320,128]{1,0:T(8,128)(2,1)S(1)} %bitcast.5), custom_call_target="tpu_custom_call" | custom-call | tf_op jit(solution)/shard_map/unpack/pallas_call | solution.py:138

commit v7 on v6

--- a/solution.py
+++ b/solution.py
@@ -57,9 +57,9 @@
     before = jnp.dot(one_hot(member), one_hot(earlier), preferred_element_type=jnp.float32)
     places = jnp.sum(jnp.where(member, before, 0.0), axis=0, keepdims=True).astype(jnp.int32)
     chosen = one_hot(rows == owners * stride + places)
-    up = jnp.transpose(jnp.concatenate([weights, jnp.zeros((7, goals), jnp.float32)], axis=0))
+    column = jnp.transpose(jnp.broadcast_to(weights, (embed_ref.shape[1], goals)))
     copies[2].wait()
-    scaled = (up[:, 0:1] * embed_ref[...].astype(jnp.float32)).astype(jnp.bfloat16)
+    scaled = (column * embed_ref[...].astype(jnp.float32)).astype(jnp.bfloat16)
     me = lax.axis_index("gy") * across + lax.axis_index("gx")
     tall = pl.cdiv(capacity, 8) * 8
     place = iota((tall, goals), 0) == places

time: 17.3 us -> 17.3 us (level)
  no operation moved by 1% of the time
where the time goes in v7:
time: 17.3 us; the launch traced here: 17.1 us
  blocking collectives  14.5 us (84%)
  Pallas kernels  1.9 us (11%)
  between operations  0.64 us (4%)
    all_to_all x1, blocking collectives, shards(): lax.all_to_all(outgoing.reshape(devices, stride // 2, 2, width), ('gy', '...  14.5 us
    pallas_call x1, Pallas kernels, shards(): pl.pallas_call(lambda *refs: pack(capacity, *refs), out_shape=jax.ShapeDt...  1.09 us
    pallas_call x1, Pallas kernels, shards(): pl.pallas_call(lambda *refs: unpack(devices, capacity, *refs), out_shape=...  0.81 us

profile of v7, /device:TPU:0, one launch (start us, length us, event | category | flops | bytes accessed | tf_op | source)
XLA Modules:
  0.0 17.1 jit_solution(11986292944244326599)
XLA Ops:
  0.6 1.1 %pack.1 = bf16[320,128]{1,0:T(8,128)(2,1)S(1)} custom-call(bf16[128,128]{1,0:T(8,128)(2,1)} %refs_0_.1, s32[1,128]{1,0:T(1,128)} %bitcast.7, f32[1,128]{1,0:T(1,128)} %bitcast.8), custom_call_target="tpu_custom_call" | custom-call | tf_op jit(solution)/shard_map/pack/pallas_call | solution.py:121
  1.7 14.5 %all_to_all.5 = bf16[32,5,2,128]{3,2,1,0:T(2,128)(2,1)S(1)} all-to-all(bf16[32,5,2,128]{3,2,1,0:T(2,128)(2,1)S(1)} %bitcast.6), channel_id=1, replica_groups=mesh['gx'=8,'gy'=4] {'gy','gx'}, dimensions={0} | all-to-all | bytes 163840 | tf_op jit(solution)/shard_map/all_to_all | solution.py:135
  16.3 0.8 %unpack.1 = (f32[64,128]{1,0:T(8,128)}, f32[1,64]{1,0:T(1,128)}) custom-call(bf16[320,128]{1,0:T(8,128)(2,1)S(1)} %bitcast.5), custom_call_target="tpu_custom_call" | custom-call | tf_op jit(solution)/shard_map/unpack/pallas_call | solution.py:138

commit v8 on v7

--- a/solution.py
+++ b/solution.py
@@ -54,8 +54,9 @@
     owners = (owners - major * along) * across + major
     member = iota((devices, goals), 0) == owners
     earlier = iota((goals, goals), 0) < iota((goals, goals), 1)
-    before = jnp.dot(one_hot(member), one_hot(earlier), preferred_element_type=jnp.float32)
-    places = jnp.sum(jnp.where(member, before, 0.0), axis=0, keepdims=True).astype(jnp.int32)
+    across_rows = jnp.transpose(jnp.broadcast_to(owners.astype(jnp.float32), (goals, goals)))
+    before = earlier & (across_rows == owners.astype(jnp.float32))
+    places = jnp.sum(jnp.where(before, 1.0, 0.0), axis=0, keepdims=True).astype(jnp.int32)
     chosen = one_hot(rows == owners * stride + places)
     column = jnp.transpose(jnp.broadcast_to(weights, (embed_ref.shape[1], goals)))
     copies[2].wait()

time: 17.3 us -> 17.3 us (level)
  no operation moved by 1% of the time
where the time goes in v8:
time: 17.3 us; the launch traced here: 17.1 us
  blocking collectives  14.5 us (84%)
  Pallas kernels  1.87 us (11%)
  between operations  0.64 us (4%)
    all_to_all x1, blocking collectives, shards(): lax.all_to_all(outgoing.reshape(devices, stride // 2, 2, width), ('gy', '...  14.5 us
    pallas_call x1, Pallas kernels, shards(): pl.pallas_call(lambda *refs: pack(capacity, *refs), out_shape=jax.ShapeDt...  1.06 us
    pallas_call x1, Pallas kernels, shards(): pl.pallas_call(lambda *refs: unpack(devices, capacity, *refs), out_shape=...  0.81 us

profile of v8, /device:TPU:0, one launch (start us, length us, event | category | flops | bytes accessed | tf_op | source)
XLA Modules:
  0.0 17.1 jit_solution(12392395597553903353)
XLA Ops:
  0.6 1.1 %pack.1 = bf16[320,128]{1,0:T(8,128)(2,1)S(1)} custom-call(bf16[128,128]{1,0:T(8,128)(2,1)} %refs_0_.1, s32[1,128]{1,0:T(1,128)} %bitcast.7, f32[1,128]{1,0:T(1,128)} %bitcast.8), custom_call_target="tpu_custom_call" | custom-call | tf_op jit(solution)/shard_map/pack/pallas_call | solution.py:122
  1.7 14.5 %all_to_all.5 = bf16[32,5,2,128]{3,2,1,0:T(2,128)(2,1)S(1)} all-to-all(bf16[32,5,2,128]{3,2,1,0:T(2,128)(2,1)S(1)} %bitcast.6), channel_id=1, replica_groups=mesh['gx'=8,'gy'=4] {'gy','gx'}, dimensions={0} | all-to-all | bytes 163840 | tf_op jit(solution)/shard_map/all_to_all | solution.py:136
  16.2 0.8 %unpack.1 = (f32[64,128]{1,0:T(8,128)}, f32[1,64]{1,0:T(1,128)}) custom-call(bf16[320,128]{1,0:T(8,128)(2,1)S(1)} %bitcast.5), custom_call_target="tpu_custom_call" | custom-call | tf_op jit(solution)/shard_map/unpack/pallas_call | solution.py:139
